TPU v7x, 32 devices: a whole 2x2x4 slice. The times are simulated.
32 devices in a mesh: ens: 2 (over y), gx: 16 (over z, x, core).
Axes of the slice: x: 2, y: 2, z: 4, core: 2. Of those that a mesh axis runs over, the one named last changes fastest.
Arguments:
- model_state: float32 [8, 4, 320, 2560], P('ens', None, 'gx'), parts along dimension 0, may hold values from -6 to 6
- driving: float32 [8, 4, 320, 2560], P('ens', None, 'gx'), parts along dimension 0, may hold values from -12 to 12
- mode_east: int32 [30], replicated, may hold values from 1 to 60, as said below
- mode_north: int32 [30], replicated, may hold values from 1 to 60, as said below
- level_class: int32 [4], replicated, may hold values from 0 to 7
- nudge_table: float32 [8, 4], replicated, may hold values from 0.05 to 0.5
Outputs:
- nudged: float32 [8, 4, 320, 2560], P('ens', None, 'gx'), parts along dimension 0
- residual_log: float32 [8, 4], P('ens'), parts along dimension 0
There are 2 independent parts, one for each index of `ens`. A program takes and returns all parts, laid end to end along the dimension named above; an argument that names none is the same for every part. Nothing has to cross between parts.
Inputs may be any that keep to these rules, and one draw needn't show every extreme that they name: `mode_east`: 30 distinct wavenumbers in increasing order, the first 1 and the last 60. `mode_north`: 30 distinct wavenumbers in increasing order, the first 1 and the last 60.
All inputs are finite; a program needn't handle non-finite values.
Results may differ from a plain program's by a relative error of at most 0.0001.
Values sent between devices are 32-bit elements; how exact they have to be, the bound alone decides.
A program may use at most 128 MiB of HBM per device.

v0:
```python
import jax
import jax.numpy as jnp
from jax import lax
from jax.sharding import PartitionSpec as P

ITERS = 4
DIFFUSION = 0.24


def extended_2(cells, sides, width):
    for axis, dim in sides:
        count = lax.axis_size(axis)
        ends = count - 1
        head = lax.slice_in_dim(cells, 0, width, axis=dim)
        tail = lax.slice_in_dim(cells, cells.shape[dim] - width, cells.shape[dim], axis=dim)
        cells = jnp.concatenate(
            [
                lax.ppermute(tail, axis, [(i, (i + 1) % count) for i in range(ends)]),
                cells,
                lax.ppermute(head, axis, [((i + 1) % count, i) for i in range(ends)]),
            ],
            axis=dim,
        )
    return cells


def sine_table(wavenums, first_cell, span_cols, grid_cells):
    places = first_cell + lax.iota(jnp.int32, span_cols) + 1
    phases = wavenums[:, None] * places[None, :] % (2 * (grid_cells + 1))
    return jnp.sin(phases.astype(jnp.float32) * (jnp.pi / (grid_cells + 1)))


def laplace(extended):
    centre = extended[:, :, 1:-1]
    padded = jnp.pad(centre, ((0, 0), (0, 0), (0, 0), (1, 1)))
    return (
        extended[:, :, 2:]
        + extended[:, :, :-2]
        + padded[:, :, :, 2:]
        + padded[:, :, :, :-2]
        - 4.0 * centre
    )


def local(model_state, driving, mode_east, mode_north, level_class, nudge_table):
    fields, levels, columns, north_cells = model_state.shape
    tiles = lax.axis_size("gx")
    first_col = lax.axis_index("gx") * columns
    total_east = columns * tiles
    scale_norm = 4.0 / ((total_east + 1) * (north_cells + 1))
    cell_count = float(levels * total_east * north_cells)
    table_north = sine_table(mode_north, 0, north_cells, north_cells)
    table_own = sine_table(mode_east, first_col, columns, total_east)
    one_hot = (level_class[:, None] == lax.iota(jnp.int32, nudge_table.shape[0])[None, :]).astype(
        jnp.float32
    )
    weights = jnp.dot(one_hot, nudge_table, precision=lax.Precision.HIGHEST).T[:, :, None, None]
    records = []
    extended = extended_2(model_state, (("gx", 2),), ITERS)
    for substep in range(ITERS):
        reach_now = ITERS - substep
        current = extended[:, :, reach_now : reach_now + columns]
        along_north = jnp.dot(
            (driving - current).reshape(-1, north_cells),
            table_north.T,
            precision=lax.Precision.HIGHEST,
        )
        along_north = along_north.reshape(fields, levels, columns, -1)
        mode_partial_value = (
            jnp.einsum("flxb,ax->flab", along_north, table_own, precision=lax.Precision.HIGHEST)
            * scale_norm
        )
        coeffs = lax.psum(mode_partial_value, "gx")
        lead_col = first_col - (reach_now - 1)
        span_cols = columns + 2 * (reach_now - 1)
        table_wide = sine_table(mode_east, lead_col, span_cols, total_east)
        global_col = lead_col + lax.iota(jnp.int32, span_cols)
        inside = ((global_col >= 0) & (global_col < total_east))[None, None, :, None]
        partial_value = jnp.einsum(
            "flab,ax->flxb", coeffs, table_wide, precision=lax.Precision.HIGHEST
        )
        rebuild_span_cols = table_wide.shape[1]
        flat = jnp.dot(
            partial_value.reshape(-1, partial_value.shape[-1]),
            table_north,
            precision=lax.Precision.HIGHEST,
        )
        updated = (
            extended[:, :, 1:-1]
            + flat.reshape(fields, levels, rebuild_span_cols, north_cells) * weights
            + DIFFUSION * laplace(extended)
        )
        extended = jnp.where(inside, updated, 0.0)
        current = extended[:, :, reach_now - 1 : reach_now - 1 + columns]
        remain = driving - current
        squares = jnp.sum(remain * remain, axis=(1, 2, 3))
        records.append(lax.psum(squares, "gx"))
    stacked = jnp.stack(records)
    return (current, jnp.sqrt(stacked / cell_count))


def solution(mesh):
    return jax.shard_map(
        local,
        mesh=mesh,
        in_specs=(P("ens", None, "gx", None), P("ens", None, "gx", None), P(), P(), P(), P()),
        out_specs=(P("ens", None, "gx", None), P("ens", None)),
        check_vma=False,
    )
```

profile of v0, /device:TPU:0, one launch (start us, length us, event | category | flops | bytes accessed | tf_op | source)
XLA Modules:
  0.0 384.4 jit_solution(12978652984436395358)
XLA Ops:
  0.7 3.1 copy.8
  3.8 1.9 copy-done.2
  5.7 1.2 fusion.219
  6.9 3.3 collective-permute-start
  10.2 1.3 collective-permute-start.1
  13.4 3.6 sub.42
  17.0 4.7 %fusion.29 = f32[4,4,20,30]{3,2,1,0:T(8,128)S(1)} fusion(f32[4,4,20,2560]{3,1,2,0:T(4,128)S(1)} %sub.42, s32[2560]{0:T(1024)S(1)} %iota_add_fusion, s32[30]{0:T(128)S(1)} %copy-done.7), kind=kOutput, calls=%fused_computation.49 | convolution fusion | flops 295603200 | bytes 3325560 | tf_op jit(solution)/shard_map/dot_general | solution.py:63
  22.3 0.9 copy.72
  23.1 66.8 %psum.56 = f32[4,4,30,30]{3,1,0,2:T(4,128)S(1)} all-reduce(f32[4,4,30,30]{3,1,0,2:T(4,128)} %bitcast.73), channel_id=1, replica_groups=mesh['ens'=2,'gx'=16] {'gx'}, use_global_device_ids=true, to_apply=%region_0.1 | all-reduce | flops 14400 | bytes 115200 | tf_op jit(solution)/shard_map/psum | solution.py:73
  91.6 3.2 pad_maximum_fusion
  94.8 0.9 slice.106
  95.7 6.8 %fusion.5 = f32[4,4,26,2560]{3,2,1,0:T(8,128)S(1)} fusion(f32[4,4,26,2560]{3,2,1,0:T(8,128)S(1)} %slice.106, f32[4,4,28,2560]{3,2,1,0:T(8,128)S(1)} %pad_maximum_fusion, f32[4,4,26,30]{3,2,1,0:T(8,128)S(1)} %convolution_bitcast_fusion, f32[4,4]{1,0:T(4,128)S(1)} %copy.11, pred[26]{0:T(512)(128)(4,1)S(1)} %compare_and_fusion, s32[2560]{0:T(1024)S(1)} %iota_add_fusion, ...), kind=kOutput, calls=%fused_computation.7 | convolution fusion | flops 394726400 | bytes 17099730 | tf_op jit(solution)/shard_map/dot_general | solution.py:83
  102.6 5.5 %fusion.32 = f32[4,4,20,30]{3,2,1,0:T(8,128)S(1)} fusion(f32[4,4,20,2560]{3,1,2,0:T(4,128)S(1)} %copy-done.1, f32[4,4,26,2560]{3,2,1,0:T(8,128)S(1)} %fusion.5, s32[2560]{0:T(1024)S(1)} %iota_add_fusion, s32[30]{0:T(128)S(1)} %copy-done.7), kind=kOutput, calls=%fused_computation.55 | convolution fusion | flops 296422400 | bytes 7260160 | tf_op jit(solution)/shard_map/dot_general | solution.py:63
  108.1 2.5 slice.109
  111.1 0.9 copy.71
  111.9 60.4 %psum.57 = f32[4,4,30,30]{3,1,0,2:T(4,128)S(1)} all-reduce(f32[4,4,30,30]{3,1,0,2:T(4,128)} %bitcast.74), channel_id=1, replica_groups=mesh['ens'=2,'gx'=16] {'gx'}, use_global_device_ids=true, to_apply=%region_1.2 | all-reduce | flops 14400 | bytes 115200 | tf_op jit(solution)/shard_map/psum | solution.py:73
  172.3 1.2 convolution_bitcast_fusion.3
  173.5 10.2 %fusion.12 = f32[4,4,24,2560]{3,2,1,0:T(8,128)S(1)} fusion(f32[4,4,24,2560]{3,2,1,0:T(8,128)} %slice.109, f32[4,4,24,30]{3,2,1,0:T(8,128)S(1)} %convolution_bitcast_fusion.3, f32[4,4,26,2560]{3,2,1,0:T(8,128)} %copy-done.5, f32[4,4]{1,0:T(4,128)S(1)} %copy.11, pred[24]{0:T(512)(128)(4,1)} %compare_and_fusion.1, s32[2560]{0:T(1024)S(1)} %iota_add_fusion, ...), kind=kOutput, calls=%fused_computation.19 | convolution fusion | flops 364416000 | bytes 15785168 | tf_op jit(solution)/shard_map/dot_general | solution.py:83
  183.7 5.2 %fusion.33 = f32[4,4,20,30]{3,2,1,0:T(8,128)S(1)} fusion(f32[4,4,20,2560]{3,1,2,0:T(4,128)S(1)} %copy-done.1, f32[4,4,24,2560]{3,2,1,0:T(8,128)S(1)} %fusion.12, s32[2560]{0:T(1024)S(1)} %iota_add_fusion, s32[30]{0:T(128)S(1)} %copy-done.7), kind=kOutput, calls=%fused_computation.56 | convolution fusion | flops 296422400 | bytes 7257720 | tf_op jit(solution)/shard_map/dot_general | solution.py:63
  189.0 2.5 slice.113
  191.9 0.9 copy.70
  192.8 60.8 %psum.58 = f32[4,4,30,30]{3,1,0,2:T(4,128)S(1)} all-reduce(f32[4,4,30,30]{3,1,0,2:T(4,128)} %bitcast.75), channel_id=1, replica_groups=mesh['ens'=2,'gx'=16] {'gx'}, use_global_device_ids=true, to_apply=%region_2.3 | all-reduce | flops 14400 | bytes 115200 | tf_op jit(solution)/shard_map/psum | solution.py:73
  253.6 1.1 convolution_bitcast_fusion.2
  254.7 9.9 %fusion.13 = f32[4,4,22,2560]{3,2,1,0:T(8,128)S(1)} fusion(f32[4,4,22,2560]{3,2,1,0:T(8,128)} %slice.113, f32[4,4,22,30]{3,2,1,0:T(8,128)S(1)} %convolution_bitcast_fusion.2, f32[4,4,24,2560]{3,2,1,0:T(8,128)} %copy-done.3, f32[4,4]{1,0:T(4,128)S(1)} %copy.11, pred[22]{0:T(512)(128)(4,1)} %compare_and_fusion.2, s32[2560]{0:T(1024)S(1)} %iota_add_fusion, ...), kind=kOutput, calls=%fused_computation.20 | convolution fusion | flops 334105600 | bytes 14470606 | tf_op jit(solution)/shard_map/dot_general | solution.py:83
  264.6 5.2 %fusion.31 = f32[4,4,20,30]{3,2,1,0:T(8,128)S(1)} fusion(f32[4,4,20,2560]{3,1,2,0:T(4,128)S(1)} %copy-done.1, s32[2560]{0:T(1024)S(1)} %iota_add_fusion, s32[30]{0:T(128)S(1)} %copy-done.7, f32[4,4,22,2560]{3,2,1,0:T(8,128)S(1)} %fusion.13), kind=kOutput, calls=%fused_computation.54 | convolution fusion | flops 296422400 | bytes 6930040 | tf_op jit(solution)/shard_map/dot_general | solution.py:63
  269.9 2.4 slice.117
  272.8 0.9 copy.69
  273.6 60.6 %psum.59 = f32[4,4,30,30]{3,1,0,2:T(4,128)S(1)} all-reduce(f32[4,4,30,30]{3,1,0,2:T(4,128)} %bitcast.76), channel_id=1, replica_groups=mesh['ens'=2,'gx'=16] {'gx'}, use_global_device_ids=true, to_apply=%region_3.4 | all-reduce | flops 14400 | bytes 115200 | tf_op jit(solution)/shard_map/psum | solution.py:73
  334.7 15.7 %multiply_reduce_fusion.2 = (f32[4]{0:T(128)S(1)}, f32[4]{0:T(128)S(1)}, f32[4]{0:T(128)S(1)}, f32[4]{0:T(128)S(1)}, f32[4,4,20,2560]{3,2,1,0:T(8,128)S(1)}) fusion(f32[4,4,26,2560]{3,2,1,0:T(8,128)} %copy-done.5, f32[4,4,20,2560]{3,1,2,0:T(4,128)S(1)} %copy-done.1, f32[4,4,24,2560]{3,2,1,0:T(8,128)} %copy-done.3, f32[4,4,22,2560]{3,2,1,0:T(8,128)} %copy-done.4, ...), kind=kOutput, calls=%fused_computation.53 | convolution fusion | flops 313625600 | bytes 26263308 | tf_op jit(solution)/shard_map/dot_general | solution.py:83
  350.4 3.8 copy.19
  354.2 29.5 %all-reduce.4 = (f32[1,4]{1,0:T(1,128)S(1)}, f32[1,4]{1,0:T(1,128)S(1)}, f32[1,4]{1,0:T(1,128)S(1)}, f32[1,4]{1,0:T(1,128)S(1)}) all-reduce(f32[1,4]{1,0:T(1,128)S(1)} %bitcast.80, f32[1,4]{1,0:T(1,128)S(1)} %bitcast.79, f32[1,4]{1,0:T(1,128)S(1)} %bitcast.78, f32[1,4]{1,0:T(1,128)S(1)} %bitcast.77), channel_id=1, replica_groups=mesh['ens'=2,'gx'=16] {'gx'}, use_global_device_ids=true, to_apply=%region_11.12 | all-reduce | flops 16 | bytes 128 | tf_op jit(solution)/shard_map/psum | solution.py:97
  383.7 0.6 fusion.164
  (36 shorter events, 6.1 us)
Async XLA Ops:
  0.6 12.5 %copy-start = (f32[8,4]{0,1:T(4,128)S(1)}, f32[8,4]{0,1:T(4,128)}, u32[]{:S(2)}) copy-start(f32[8,4]{0,1:T(4,128)} %param.11) | copy-start | bytes 388
  0.6 12.4 %copy-start.8 = (s32[4]{0:T(128)S(1)}, s32[4]{0:T(128)}, u32[]{:S(2)}) copy-start(s32[4]{0:T(128)} %param.10) | copy-start | bytes 52
  0.7 12.7 %copy-start.1 = (f32[4,4,20,2560]{3,1,2,0:T(4,128)S(1)}, f32[4,4,20,2560]{3,1,2,0:T(4,128)}, u32[]{:S(2)}) copy-start(f32[4,4,20,2560]{3,1,2,0:T(4,128)} %param.7) | copy-start | bytes 9830404
  3.8 1.9 copy-start.2
  6.9 84.6 %collective-permute-start = (f32[4,4,4,2560]{3,2,1,0:T(4,128)}, f32[4,4,4,2560]{3,2,1,0:T(4,128)}, u32[]{:S(2)}, u32[]{:S(2)}) collective-permute-start(f32[4,4,4,2560]{3,2,1,0:T(4,128)} %get-tuple-element.12), channel_id=1, source_target_pairs={{0,1},{1,2},{2,3},{3,4},{4,5},{5,6},{6,7},{7,8},{8,9},{9,10},{10,1... | collective-permute-start | bytes 1966088 | tf_op jit(solution)/shard_map/ppermute | solution.py:18
  10.2 81.4 %collective-permute-start.1 = (f32[4,4,4,2560]{3,2,1,0:T(4,128)}, f32[4,4,4,2560]{3,2,1,0:T(4,128)}, u32[]{:S(2)}, u32[]{:S(2)}) collective-permute-start(f32[4,4,4,2560]{3,2,1,0:T(4,128)} %get-tuple-element.13), channel_id=1, source_target_pairs={{1,0},{2,1},{3,2},{4,3},{5,4},{6,5},{7,6},{8,7},{9,8},{10,9},{11,1... | collective-permute-start | bytes 1966088 | tf_op jit(solution)/shard_map/ppermute | solution.py:20
  13.4 3.6 copy-start.7
  17.0 4.8 %copy-start.6 = (s32[30]{0:T(128)S(1)}, s32[30]{0:T(128)}, u32[]{:S(2)}) copy-start(s32[30]{0:T(128)} %param.8) | copy-start | bytes 364
  102.6 5.5 %copy-start.5 = (f32[4,4,26,2560]{3,2,1,0:T(8,128)}, f32[4,4,26,2560]{3,2,1,0:T(8,128)S(1)}, u32[]{:S(2)}) copy-start(f32[4,4,26,2560]{3,2,1,0:T(8,128)S(1)} %fusion.5) | copy-start | bytes 12779524
  183.7 5.2 %copy-start.3 = (f32[4,4,24,2560]{3,2,1,0:T(8,128)}, f32[4,4,24,2560]{3,2,1,0:T(8,128)S(1)}, u32[]{:S(2)}) copy-start(f32[4,4,24,2560]{3,2,1,0:T(8,128)S(1)} %fusion.12) | copy-start | bytes 11796484
  264.6 5.3 %copy-start.4 = (f32[4,4,22,2560]{3,2,1,0:T(8,128)}, f32[4,4,22,2560]{3,2,1,0:T(8,128)S(1)}, u32[]{:S(2)}) copy-start(f32[4,4,22,2560]{3,2,1,0:T(8,128)S(1)} %fusion.13) | copy-start | bytes 10813444
where the time goes:
time: 392 us; the launch traced here: 384 us
  blocking collectives  278 us (71%)
  matrix products  68.8 us (18%)
  local copies, waits for them, and re-layouts  21.9 us (6%)
  other arithmetic  10.1 us (3%)
  starting transfers between devices  4.53 us (1%)
    psum x4, blocking collectives, local(): coeffs = lax.psum(mode_partial_value, 'gx')  248 us
    dot_general x4, matrix products, local(): jnp.dot(partial_value.reshape(-1, partial_value.shape[-1]), table_north,...  42.6 us
    psum x1, blocking collectives, local(): records.append(lax.psum(squares, 'gx'))  29.5 us
    dot_general x4, matrix products, local(): jnp.dot((driving - current).reshape(-1, north_cells), table_north.T, prec...  20.7 us
    unnamed x24, local copies, waits for them, and re-layouts  12.3 us
    slice x4, local copies, waits for them, and re-layouts, local(): extended[:, :, 1:-1]  8.25 us
  transfers between devices with their start and end apart: 2, of which 0 were waited for; matrix products, arithmetic and copies ran while one was open for 3% of the time, Pallas kernels for 0%

commit v1 on v0

--- a/solution.py
+++ b/solution.py
@@ -70,7 +70,7 @@
             jnp.einsum("flxb,ax->flab", along_north, table_own, precision=lax.Precision.HIGHEST)
             * scale_norm
         )
-        coeffs = lax.psum(mode_partial_value, "gx")
+        coeffs = jnp.sum(lax.all_gather(mode_partial_value, "gx"), axis=0)
         lead_col = first_col - (reach_now - 1)
         span_cols = columns + 2 * (reach_now - 1)
         table_wide = sine_table(mode_east, lead_col, span_cols, total_east)

time: 392 us -> 358 us (0.913)
  blocking collectives: 278 us -> 237 us
  other arithmetic: 10.1 us -> 21.6 us
    psum x4 -> x0, blocking collectives: 248 us -> none  [local(): coeffs = lax.psum(mode_partial_value, 'gx')]
    all_gather x0 -> x4, blocking collectives: none -> 207 us  [local(): coeffs = jnp.sum(lax.all_gather(mode_partial_value, 'gx'), axis=0)]
    reduce_sum x0 -> x4, other arithmetic: none -> 11.9 us  [local(): coeffs = jnp.sum(lax.all_gather(mode_partial_value, 'gx'), axis=0)]
  transfers between devices with their start and end apart: 2 -> 2, of which waited for: 0 -> 0; matrix products, arithmetic and copies ran while one was open for 3% -> 4% of each run, Pallas kernels for 0% -> 0%
where the time goes in v1:
time: 358 us; the launch traced here: 352 us
  blocking collectives  237 us (66%)
  matrix products  68.3 us (19%)
  other arithmetic  21.6 us (6%)
  local copies, waits for them, and re-layouts  19.1 us (5%)
  starting transfers between devices  4.55 us (1%)
    all_gather x4, blocking collectives, local(): coeffs = jnp.sum(lax.all_gather(mode_partial_value, 'gx'), axis=0)  207 us
    dot_general x4, matrix products, local(): jnp.dot(partial_value.reshape(-1, partial_value.shape[-1]), table_north,...  42.6 us
    psum x1, blocking collectives, local(): records.append(lax.psum(squares, 'gx'))  30.6 us
    dot_general x4, matrix products, local(): jnp.dot((driving - current).reshape(-1, north_cells), table_north.T, prec...  20.8 us
    reduce_sum x4, other arithmetic, local(): coeffs = jnp.sum(lax.all_gather(mode_partial_value, 'gx'), axis=0)  11.9 us
    unnamed x24, local copies, waits for them, and re-layouts  8.86 us
    slice x4, local copies, waits for them, and re-layouts, local(): extended[:, :, 1:-1]  8.25 us
  transfers between devices with their start and end apart: 2, of which 0 were waited for; matrix products, arithmetic and copies ran while one was open for 4% of the time, Pallas kernels for 0%

profile of v1, /device:TPU:0, one launch (start us, length us, event | category | flops | bytes accessed | tf_op | source)
XLA Modules:
  0.0 352.2 jit_solution(11070941493842399604)
XLA Ops:
  0.7 3.1 copy.36
  3.8 1.9 copy-done.3
  5.7 1.2 fusion.223
  6.9 3.3 collective-permute-start
  10.2 1.3 collective-permute-start.1
  12.9 3.6 %sub.42 = f32[4,4,20,2560]{3,1,2,0:T(4,128)S(1)} subtract(f32[4,4,20,2560]{3,1,2,0:T(4,128)S(1)} %copy-done.2, f32[4,4,20,2560]{3,1,2,0:T(4,128)} %param.6) | non-fusion elementwise | flops 819200 | bytes 9830400 | tf_op jit(solution)/shard_map/sub | solution.py:64
  16.5 4.7 %fusion.29 = f32[4,4,20,30]{3,2,1,0:T(8,128)S(1)} fusion(f32[4,4,20,2560]{3,1,2,0:T(4,128)S(1)} %sub.42, s32[2560]{0:T(1024)S(1)} %iota_add_fusion, s32[30]{0:T(128)S(1)} %copy-done.8), kind=kOutput, calls=%fused_computation.49 | convolution fusion | flops 295603200 | bytes 3325560 | tf_op jit(solution)/shard_map/dot_general | solution.py:63
  22.0 53.3 %all-gather = f32[64,4,30,30]{3,1,2,0:T(4,128)} all-gather(f32[4,4,30,30]{3,1,2,0:T(4,128)S(1)} %copy.40), channel_id=2, replica_groups=mesh['ens'=2,'gx'=16] {'gx'}, dimensions={0}, use_global_device_ids=true | all-gather | bytes 979200 | tf_op jit(solution)/shard_map/all_gather | solution.py:73
  75.3 3.0 reduce_sum.72
  78.3 0.6 compare_and_fusion.1
  80.0 3.2 pad_maximum_fusion
  83.2 0.9 slice.106
  84.1 6.8 %fusion.5 = f32[4,4,26,2560]{3,2,1,0:T(8,128)S(1)} fusion(f32[4,4,26,2560]{3,2,1,0:T(8,128)S(1)} %slice.106, f32[4,4,28,2560]{3,2,1,0:T(8,128)S(1)} %pad_maximum_fusion, f32[4,4,26,30]{3,2,1,0:T(8,128)S(1)} %convolution_bitcast_fusion, f32[4,4]{1,0:T(4,128)S(1)} %copy.42, pred[26]{0:T(512)(128)(4,1)S(1)} %compare_and_fusion, s32[2560]{0:T(1024)S(1)} %iota_add_fusion, ...), kind=kOutput, calls=%fused_computation.7 | convolution fusion | flops 394726400 | bytes 17099730 | tf_op jit(solution)/shard_map/dot_general | solution.py:83
  91.0 5.6 %fusion.32 = f32[4,4,20,30]{3,2,1,0:T(8,128)S(1)} fusion(f32[4,4,20,2560]{3,1,2,0:T(4,128)S(1)} %copy-done.2, f32[4,4,26,2560]{3,2,1,0:T(8,128)S(1)} %fusion.5, s32[2560]{0:T(1024)S(1)} %iota_add_fusion, s32[30]{0:T(128)S(1)} %copy-done.8), kind=kOutput, calls=%fused_computation.55 | convolution fusion | flops 296422400 | bytes 7260160 | tf_op jit(solution)/shard_map/dot_general | solution.py:63
  96.6 2.5 slice.109
  99.8 48.5 %all-gather.1 = f32[64,4,30,30]{3,1,2,0:T(4,128)} all-gather(f32[4,4,30,30]{3,1,2,0:T(4,128)S(1)} %copy.44), channel_id=3, replica_groups=mesh['ens'=2,'gx'=16] {'gx'}, dimensions={0}, use_global_device_ids=true | all-gather | bytes 979200 | tf_op jit(solution)/shard_map/all_gather | solution.py:73
  148.3 3.0 reduce_sum.73
  151.3 1.1 convolution_bitcast_fusion.3
  152.4 10.2 %fusion.12 = f32[4,4,24,2560]{3,2,1,0:T(8,128)S(1)} fusion(f32[4,4,24,2560]{3,2,1,0:T(8,128)} %slice.109, f32[4,4,24,30]{3,2,1,0:T(8,128)S(1)} %convolution_bitcast_fusion.3, f32[4,4,26,2560]{3,2,1,0:T(8,128)} %copy-done.6, f32[4,4]{1,0:T(4,128)S(1)} %copy.42, pred[24]{0:T(512)(128)(4,1)} %compare_and_fusion.1, s32[2560]{0:T(1024)S(1)} %iota_add_fusion, ...), kind=kOutput, calls=%fused_computation.19 | convolution fusion | flops 364416000 | bytes 15785168 | tf_op jit(solution)/shard_map/dot_general | solution.py:83
  162.6 5.2 %fusion.33 = f32[4,4,20,30]{3,2,1,0:T(8,128)S(1)} fusion(f32[4,4,20,2560]{3,1,2,0:T(4,128)S(1)} %copy-done.2, f32[4,4,24,2560]{3,2,1,0:T(8,128)S(1)} %fusion.12, s32[2560]{0:T(1024)S(1)} %iota_add_fusion, s32[30]{0:T(128)S(1)} %copy-done.8), kind=kOutput, calls=%fused_computation.56 | convolution fusion | flops 296422400 | bytes 7257720 | tf_op jit(solution)/shard_map/dot_general | solution.py:63
  167.9 2.5 slice.113
  171.0 54.7 %all-gather.2 = f32[64,4,30,30]{3,1,2,0:T(4,128)} all-gather(f32[4,4,30,30]{3,1,2,0:T(4,128)S(1)} %copy.48), channel_id=4, replica_groups=mesh['ens'=2,'gx'=16] {'gx'}, dimensions={0}, use_global_device_ids=true | all-gather | bytes 979200 | tf_op jit(solution)/shard_map/all_gather | solution.py:73
  225.8 3.0 reduce_sum.74
  229.2 9.9 %fusion.13 = f32[4,4,22,2560]{3,2,1,0:T(8,128)S(1)} fusion(f32[4,4,22,2560]{3,2,1,0:T(8,128)} %slice.113, f32[4,4,22,30]{3,2,1,0:T(8,128)S(1)} %convolution_bitcast_fusion.2, f32[4,4,24,2560]{3,2,1,0:T(8,128)} %copy-done.4, f32[4,4]{1,0:T(4,128)S(1)} %copy.42, pred[22]{0:T(512)(128)(4,1)} %compare_and_fusion.2, s32[2560]{0:T(1024)S(1)} %iota_add_fusion, ...), kind=kOutput, calls=%fused_computation.20 | convolution fusion | flops 334105600 | bytes 14470606 | tf_op jit(solution)/shard_map/dot_general | solution.py:83
  239.1 5.2 %fusion.31 = f32[4,4,20,30]{3,2,1,0:T(8,128)S(1)} fusion(f32[4,4,20,2560]{3,1,2,0:T(4,128)S(1)} %copy-done.2, s32[2560]{0:T(1024)S(1)} %iota_add_fusion, s32[30]{0:T(128)S(1)} %copy-done.8, f32[4,4,22,2560]{3,2,1,0:T(8,128)S(1)} %fusion.13), kind=kOutput, calls=%fused_computation.54 | convolution fusion | flops 296422400 | bytes 6930040 | tf_op jit(solution)/shard_map/dot_general | solution.py:63
  244.4 2.4 slice.117
  247.5 50.4 %all-gather.3 = f32[64,4,30,30]{3,1,2,0:T(4,128)} all-gather(f32[4,4,30,30]{3,1,2,0:T(4,128)S(1)} %copy.52), channel_id=5, replica_groups=mesh['ens'=2,'gx'=16] {'gx'}, dimensions={0}, use_global_device_ids=true | all-gather | bytes 979200 | tf_op jit(solution)/shard_map/all_gather | solution.py:73
  297.9 3.0 reduce_sum.75
  301.3 15.6 %multiply_reduce_fusion.2 = (f32[4]{0:T(128)S(1)}, f32[4]{0:T(128)S(1)}, f32[4]{0:T(128)S(1)}, f32[4]{0:T(128)S(1)}, f32[4,4,20,2560]{3,2,1,0:T(8,128)S(1)}) fusion(f32[4,4,26,2560]{3,2,1,0:T(8,128)} %copy-done.6, f32[4,4,20,2560]{3,1,2,0:T(4,128)S(1)} %copy-done.2, f32[4,4,24,2560]{3,2,1,0:T(8,128)} %copy-done.4, f32[4,4,22,2560]{3,2,1,0:T(8,128)} %copy-done.5, ...), kind=kOutput, calls=%fused_computation.53 | convolution fusion | flops 313625600 | bytes 26263308 | tf_op jit(solution)/shard_map/dot_general | solution.py:83
  317.0 3.8 %copy.56 = f32[4,4,20,2560]{3,1,2,0:T(4,128)} copy(f32[4,4,20,2560]{3,2,1,0:T(8,128)S(1)} %get-tuple-element.18) | data formatting | bytes 6553600
  320.8 30.6 %all-reduce.4 = (f32[1,4]{1,0:T(1,128)S(1)}, f32[1,4]{1,0:T(1,128)S(1)}, f32[1,4]{1,0:T(1,128)S(1)}, f32[1,4]{1,0:T(1,128)S(1)}) all-reduce(f32[1,4]{1,0:T(1,128)S(1)} %bitcast.80, f32[1,4]{1,0:T(1,128)S(1)} %bitcast.79, f32[1,4]{1,0:T(1,128)S(1)} %bitcast.78, f32[1,4]{1,0:T(1,128)S(1)} %bitcast.77), channel_id=1, replica_groups=mesh['ens'=2,'gx'=16] {'gx'}, use_global_device_ids=true, to_apply=%region_11.12 | all-reduce | flops 16 | bytes 128 | tf_op jit(solution)/shard_map/psum | solution.py:97
  351.3 0.6 fusion.168
  (44 shorter events, 6.2 us)
Async XLA Ops:
  0.6 12.0 %copy-start = (f32[8,4]{0,1:T(4,128)S(1)}, f32[8,4]{0,1:T(4,128)}, u32[]{:S(2)}) copy-start(f32[8,4]{0,1:T(4,128)} %param.11) | copy-start | bytes 388
  0.6 12.0 %copy-start.9 = (s32[4]{0:T(128)S(1)}, s32[4]{0:T(128)}, u32[]{:S(2)}) copy-start(s32[4]{0:T(128)} %param.10) | copy-start | bytes 52
  0.7 12.2 %copy-start.2 = (f32[4,4,20,2560]{3,1,2,0:T(4,128)S(1)}, f32[4,4,20,2560]{3,1,2,0:T(4,128)}, u32[]{:S(2)}) copy-start(f32[4,4,20,2560]{3,1,2,0:T(4,128)} %param.7) | copy-start | bytes 9830404
  3.8 1.9 copy-start.3
  6.9 73.0 %collective-permute-start = (f32[4,4,4,2560]{3,2,1,0:T(4,128)}, f32[4,4,4,2560]{3,2,1,0:T(4,128)}, u32[]{:S(2)}, u32[]{:S(2)}) collective-permute-start(f32[4,4,4,2560]{3,2,1,0:T(4,128)} %get-tuple-element.16), channel_id=1, source_target_pairs={{0,1},{1,2},{2,3},{3,4},{4,5},{5,6},{6,7},{7,8},{8,9},{9,10},{10,1... | collective-permute-start | bytes 1966088 | tf_op jit(solution)/shard_map/ppermute | solution.py:18
  10.2 69.8 %collective-permute-start.1 = (f32[4,4,4,2560]{3,2,1,0:T(4,128)}, f32[4,4,4,2560]{3,2,1,0:T(4,128)}, u32[]{:S(2)}, u32[]{:S(2)}) collective-permute-start(f32[4,4,4,2560]{3,2,1,0:T(4,128)} %get-tuple-element.17), channel_id=1, source_target_pairs={{1,0},{2,1},{3,2},{4,3},{5,4},{6,5},{7,6},{8,7},{9,8},{10,9},{11,1... | collective-permute-start | bytes 1966088 | tf_op jit(solution)/shard_map/ppermute | solution.py:20
  12.9 3.6 %copy-start.8 = (s32[30]{0:T(128)S(1)}, s32[30]{0:T(128)}, u32[]{:S(2)}) copy-start(s32[30]{0:T(128)} %param.9) | copy-start | bytes 364
  16.5 4.8 %copy-start.7 = (s32[30]{0:T(128)S(1)}, s32[30]{0:T(128)}, u32[]{:S(2)}) copy-start(s32[30]{0:T(128)} %param.8) | copy-start | bytes 364
  91.0 5.7 %copy-start.6 = (f32[4,4,26,2560]{3,2,1,0:T(8,128)}, f32[4,4,26,2560]{3,2,1,0:T(8,128)S(1)}, u32[]{:S(2)}) copy-start(f32[4,4,26,2560]{3,2,1,0:T(8,128)S(1)} %fusion.5) | copy-start | bytes 12779524
  162.6 5.2 %copy-start.4 = (f32[4,4,24,2560]{3,2,1,0:T(8,128)}, f32[4,4,24,2560]{3,2,1,0:T(8,128)S(1)}, u32[]{:S(2)}) copy-start(f32[4,4,24,2560]{3,2,1,0:T(8,128)S(1)} %fusion.12) | copy-start | bytes 11796484
  239.1 5.3 %copy-start.5 = (f32[4,4,22,2560]{3,2,1,0:T(8,128)}, f32[4,4,22,2560]{3,2,1,0:T(8,128)S(1)}, u32[]{:S(2)}) copy-start(f32[4,4,22,2560]{3,2,1,0:T(8,128)S(1)} %fusion.13) | copy-start | bytes 10813444
  247.5 53.8 %copy-start.10 = (pred[20]{0:T(512)(128)(4,1)S(1)}, pred[20]{0:T(512)(128)(4,1)}, u32[]{:S(2)}) copy-start(pred[20]{0:T(512)(128)(4,1)} %compare_and_fusion.3) | copy-start | bytes 64
  301.3 50.6 %copy-start.1 = (f32[8,4]{0,1:T(4,128)S(1)}, f32[8,4]{0,1:T(4,128)}, u32[]{:S(2)}) copy-start(f32[8,4]{0,1:T(4,128)} %param.11) | copy-start | bytes 388
